TPU v7x, 32 devices: a whole 2x2x4 slice. The times are simulated.
32 devices in a mesh: dp: 16 (over z, x, core), seq: 2 (over y).
Axes of the slice: x: 2, y: 2, z: 4, core: 2. Of those that a mesh axis runs over, the one named last changes fastest.
Arguments:
- tokens: float32 [16384, 1024], P(('dp', 'seq')), may hold values from -6 to 6
- lengths: int32 [16, 1], P('dp'), may hold values from 1024 to 1024, as said below
- attn_gain: bfloat16 [1024], P('dp'), may hold values from 0.5 to 1.5
- w_query: bfloat16 [1024, 1024], P('dp'), may hold values from -0.1875 to 0.1875
- w_key: bfloat16 [1024, 512], P('dp'), may hold values from -0.1875 to 0.1875
- w_value: bfloat16 [1024, 512], P('dp'), may hold values from -0.1875 to 0.1875
- query_gain: bfloat16 [64], P('dp'), may hold values from 1 to 2
- key_gain: bfloat16 [64], P('dp'), may hold values from 0.5 to 1.5
- w_out: bfloat16 [1024, 1024], P('dp'), may hold values from -1.5 to 1.5
- ffn_gain: bfloat16 [1024], P('dp'), may hold values from 0.5 to 1.5
- w_gate: bfloat16 [1024, 4608], P('dp'), may hold values from -0.1875 to 0.1875
- w_up: bfloat16 [1024, 4608], P('dp'), may hold values from -0.1875 to 0.1875
- w_down: bfloat16 [4608, 1024], P('dp'), may hold values from -0.09375 to 0.09375
- cotangent: float32 [16384, 1024], P(('dp', 'seq')), may hold values from -6 to 6
Outputs:
- block_out: float32 [16384, 1024], P(('dp', 'seq'))
- d_tokens: float32 [16384, 1024], P(('dp', 'seq'))
- d_attn_gain: float32 [1024], P('dp')
- d_w_query: float32 [1024, 1024], P('dp')
- d_w_key: float32 [1024, 512], P('dp')
- d_w_value: float32 [1024, 512], P('dp')
- d_query_gain: float32 [64], P('dp')
- d_key_gain: float32 [64], P('dp')
- d_w_out: float32 [1024, 1024], P('dp')
- d_ffn_gain: float32 [1024], P('dp')
- d_w_gate: float32 [1024, 4608], P('dp')
- d_w_up: float32 [1024, 4608], P('dp')
- d_w_down: float32 [4608, 1024], P('dp')
Inputs may be any that keep to these rules, and one draw needn't show every extreme that they name: `lengths`: every length is at least 1024; in every draw one pack, drawn from the seed, has every sequence of length 1024 and no padding.
All inputs are finite; a program needn't handle non-finite values.
Results may differ from a plain program's by a relative error of at most 0.02.
Values may be sent and summed in bfloat16 or wider, within the bound.
No kernel may reach another device: no remote copies, remote signals or barrier semaphores. Data moves between devices by JAX's collectives and lax.ppermute only.
A program may use at most 192 MiB of HBM per device.

v0:
```python
from functools import partial
import math
import jax
import jax.numpy as jnp
from jax import lax
from jax.sharding import PartitionSpec as P

H = 16
KV = 8
HD = 64
EPSILON = 1e-05
ROPE_BASE = 1000000.0
MASKED_SCORE = -1e30


def rms_norm(values, gain_vec):
    return (
        values * lax.rsqrt(jnp.mean(values * values, axis=-1, keepdims=True) + EPSILON) * gain_vec
    )


def rope_tables(positions, head_size):
    half_size = head_size // 2
    freqs = ROPE_BASE ** (-(jnp.arange(half_size, dtype=jnp.float32) * (2.0 / head_size)))
    angles = positions.astype(jnp.float32)[:, None] * freqs[None, :]
    return (jnp.cos(angles), jnp.sin(angles))


def rotate(values, cos_tab, sin_tab):
    half_size = values.shape[-1] // 2
    first = values[..., :half_size]
    second = values[..., half_size:]
    cos_b = cos_tab[:, None, :]
    sin_b = sin_tab[:, None, :]
    return jnp.concatenate(
        [first * cos_b - second * sin_b, second * cos_b + first * sin_b], axis=-1
    )


def qk_prep(linear, gain_vec, cos_tab, sin_tab, heads):
    shaped = linear.reshape(linear.shape[0], heads, -1)
    return rotate(rms_norm(shaped, gain_vec), cos_tab, sin_tab)


def swiglu(gate_act, up_act):
    return jax.nn.silu(gate_act) * up_act


def pack_layout(seq_lens, total):
    places = jnp.arange(total, dtype=jnp.int32)
    ends = jnp.cumsum(seq_lens)
    starts = ends - seq_lens
    segment = jnp.sum((places[:, None] >= ends[None, :]).astype(jnp.int32), axis=1)
    starts_ext = jnp.concatenate([starts, ends[-1:]])
    labels = jnp.arange(seq_lens.shape[0] + 1, dtype=jnp.int32)
    offset = jnp.sum(jnp.where(segment[:, None] == labels[None, :], starts_ext[None, :], 0), axis=1)
    return (places, segment, places - offset, segment < seq_lens.shape[0])


def mat_dot(form, left, right):
    return jnp.einsum(form, left, right, preferred_element_type=jnp.float32)


def body(
    tokens,
    lengths,
    attn_gain,
    w_query,
    w_key,
    w_value,
    query_gain,
    key_gain,
    w_out,
    ffn_gain,
    w_gate,
    w_up,
    w_down,
    cotangent,
):
    seq_count = lax.axis_size("seq")
    seq_rank = lax.axis_index("seq")
    tok_rows = tokens.shape[0]
    pack_len = tok_rows * seq_count
    local_kv = KV // seq_count
    group = H // KV
    local_q = local_kv * group
    score_scale = 1.0 / math.sqrt(HD)
    blk_rows = min(512, pack_len)
    blocks = pack_len // blk_rows
    places, segment, positions, valid = pack_layout(lengths[0], pack_len)
    first_row = seq_rank * tok_rows
    my_pos = lax.dynamic_slice_in_dim(positions, first_row, tok_rows)
    my_valid = lax.dynamic_slice_in_dim(valid, first_row, tok_rows).astype(jnp.float32)[:, None]
    gain_attn, query_full, key_full, value_full, gain_query, gain_key, out_full = (
        lax.all_gather(attn_gain, "dp", axis=0, tiled=True),
        lax.all_gather(w_query, "dp", axis=0, tiled=True),
        lax.all_gather(w_key, "dp", axis=0, tiled=True),
        lax.all_gather(w_value, "dp", axis=0, tiled=True),
        lax.all_gather(query_gain, "dp", axis=0, tiled=True),
        lax.all_gather(key_gain, "dp", axis=0, tiled=True),
        lax.all_gather(w_out, "dp", axis=0, tiled=True),
    )
    gain_ffn, gate_full, up_full, down_full = (
        lax.all_gather(ffn_gain, "dp", axis=0, tiled=True),
        lax.all_gather(w_gate, "dp", axis=0, tiled=True),
        lax.all_gather(w_up, "dp", axis=0, tiled=True),
        lax.all_gather(w_down, "dp", axis=0, tiled=True),
    )
    normed, pull_attn_norm = jax.vjp(rms_norm, tokens, gain_attn.astype(jnp.float32))
    normed_low = normed.astype(jnp.bfloat16)
    q_lin = jnp.dot(normed_low, query_full, preferred_element_type=jnp.float32)
    k_lin = jnp.dot(normed_low, key_full, preferred_element_type=jnp.float32)
    v_lin = jnp.dot(normed_low, value_full, preferred_element_type=jnp.float32)
    cos_tab, sin_tab = rope_tables(my_pos, HD)
    queries, pull_query = jax.vjp(
        partial(qk_prep, cos_tab=cos_tab, sin_tab=sin_tab, heads=H),
        q_lin,
        gain_query.astype(jnp.float32),
    )
    key_rows, pull_key = jax.vjp(
        partial(qk_prep, cos_tab=cos_tab, sin_tab=sin_tab, heads=KV),
        k_lin,
        gain_key.astype(jnp.float32),
    )
    q_heads, k_heads, v_heads = (
        lax.all_to_all(
            queries.astype(jnp.bfloat16).reshape(tok_rows, seq_count, -1),
            "seq",
            split_axis=1,
            concat_axis=0,
            tiled=True,
        ),
        lax.all_to_all(
            key_rows.astype(jnp.bfloat16).reshape(tok_rows, seq_count, -1),
            "seq",
            split_axis=1,
            concat_axis=0,
            tiled=True,
        ),
        lax.all_to_all(
            v_lin.astype(jnp.bfloat16).reshape(tok_rows, seq_count, -1),
            "seq",
            split_axis=1,
            concat_axis=0,
            tiled=True,
        ),
    )
    query_blocks = q_heads.reshape(blocks, blk_rows, local_kv, group, HD)
    key_all = k_heads.reshape(pack_len, local_kv, HD)
    value_all = v_heads.reshape(pack_len, local_kv, HD)
    seg_blocks = segment.reshape(blocks, blk_rows)
    place_blocks = places.reshape(blocks, blk_rows)

    def scores_of(query_blk, seg_blk, place_blk):
        scores = mat_dot("qkgd,skd->kgqs", query_blk, key_all) * score_scale
        allowed = (seg_blk[:, None] == segment[None, :]) & (places[None, :] <= place_blk[:, None])
        return jnp.where(allowed[None, None], scores, MASKED_SCORE)

    def forward_block(inputs):
        query_blk, seg_blk, place_blk = inputs
        scores = scores_of(query_blk, seg_blk, place_blk)
        top_val = jnp.max(scores, axis=-1, keepdims=True)
        expo = jnp.exp(scores - top_val)
        total = jnp.sum(expo, axis=-1, keepdims=True)
        probs = (expo / total).astype(jnp.bfloat16)
        attended_blk = mat_dot("kgqs,skd->qkgd", probs, value_all)
        return (attended_blk, (top_val + jnp.log(total))[..., 0])

    attended_heads, log_sums = lax.map(forward_block, (query_blocks, seg_blocks, place_blocks))
    attended_send = attended_heads.reshape(pack_len, 1, local_q * HD).astype(jnp.bfloat16)
    attended = lax.all_to_all(
        attended_send, "seq", split_axis=0, concat_axis=1, tiled=True
    ).reshape(tok_rows, -1)
    resid = tokens + jnp.dot(attended, out_full, preferred_element_type=jnp.float32)
    ffn_in, pull_ffn_norm = jax.vjp(rms_norm, resid, gain_ffn.astype(jnp.float32))
    ffn_low = ffn_in.astype(jnp.bfloat16)
    gate_act = jnp.dot(ffn_low, gate_full, preferred_element_type=jnp.float32)
    up_act = jnp.dot(ffn_low, up_full, preferred_element_type=jnp.float32)
    hidden, pull_swiglu = jax.vjp(swiglu, gate_act, up_act)
    hidden_low = hidden.astype(jnp.bfloat16)
    block_out = (
        resid + jnp.dot(hidden_low, down_full, preferred_element_type=jnp.float32)
    ) * my_valid
    query_back, key_back, value_back, out_back = (
        lax.all_gather(w_query, "dp", axis=0, tiled=True),
        lax.all_gather(w_key, "dp", axis=0, tiled=True),
        lax.all_gather(w_value, "dp", axis=0, tiled=True),
        lax.all_gather(w_out, "dp", axis=0, tiled=True),
    )
    gate_back, up_back, down_back = (
        lax.all_gather(w_gate, "dp", axis=0, tiled=True),
        lax.all_gather(w_up, "dp", axis=0, tiled=True),
        lax.all_gather(w_down, "dp", axis=0, tiled=True),
    )
    grad = cotangent * my_valid
    grad_low = grad.astype(jnp.bfloat16)
    d_down = mat_dot("tf,td->fd", hidden_low, grad_low)
    d_hidden = mat_dot("td,fd->tf", grad_low, down_back)
    d_gate, d_up = pull_swiglu(d_hidden)
    d_gate_low = d_gate.astype(jnp.bfloat16)
    d_up_low = d_up.astype(jnp.bfloat16)
    d_gate_w = mat_dot("td,tf->df", ffn_low, d_gate_low)
    d_up_w = mat_dot("td,tf->df", ffn_low, d_up_low)
    d_ffn = mat_dot("tf,df->td", d_gate_low, gate_back) + mat_dot("tf,df->td", d_up_low, up_back)
    d_resid_norm, d_gain_ffn = pull_ffn_norm(d_ffn)
    ffn_shards = (
        lax.psum_scatter(d_gain_ffn, "dp", scatter_dimension=0, tiled=True),
        lax.psum_scatter(d_gate_w, "dp", scatter_dimension=0, tiled=True),
        lax.psum_scatter(d_up_w, "dp", scatter_dimension=0, tiled=True),
        lax.psum_scatter(d_down, "dp", scatter_dimension=0, tiled=True),
    )
    d_resid = grad + d_resid_norm
    resid_low = d_resid.astype(jnp.bfloat16)
    d_out_w = mat_dot("tq,td->qd", attended, resid_low)
    d_attended = mat_dot("td,qd->tq", resid_low, out_back).astype(jnp.bfloat16)
    d_att_heads = lax.all_to_all(
        d_attended.reshape(tok_rows, seq_count, -1), "seq", split_axis=1, concat_axis=0, tiled=True
    )
    d_att_blocks = d_att_heads.reshape(blocks, blk_rows, local_kv, group, HD)

    def backward_block(carry, inputs):
        d_key_acc, d_value_acc = carry
        query_blk, seg_blk, place_blk, log_sum, d_att_blk = inputs
        scores = scores_of(query_blk, seg_blk, place_blk)
        probs = jnp.exp(scores - log_sum[..., None])
        d_value_acc = d_value_acc + mat_dot("kgqs,qkgd->skd", probs.astype(jnp.bfloat16), d_att_blk)
        d_probs = mat_dot("qkgd,skd->kgqs", d_att_blk, value_all)
        delta = jnp.sum(probs * d_probs, axis=-1, keepdims=True)
        d_scores = (probs * (d_probs - delta)).astype(jnp.bfloat16)
        d_query_blk = mat_dot("kgqs,skd->qkgd", d_scores, key_all) * score_scale
        d_key_acc = d_key_acc + mat_dot("kgqs,qkgd->skd", d_scores, query_blk) * score_scale
        return ((d_key_acc, d_value_acc), d_query_blk)

    zero_kv = jnp.zeros((pack_len, local_kv, HD), jnp.float32)
    (d_key_all, d_value_all), d_query_all = lax.scan(
        backward_block,
        (zero_kv, zero_kv),
        (query_blocks, seg_blocks, place_blocks, log_sums, d_att_blocks),
    )
    d_q_tok, d_k_tok, d_v_tok = (
        lax.all_to_all(
            d_query_all.reshape(pack_len, 1, -1).astype(jnp.bfloat16),
            "seq",
            split_axis=0,
            concat_axis=1,
            tiled=True,
        ),
        lax.all_to_all(
            d_key_all.reshape(pack_len, 1, -1).astype(jnp.bfloat16),
            "seq",
            split_axis=0,
            concat_axis=1,
            tiled=True,
        ),
        lax.all_to_all(
            d_value_all.reshape(pack_len, 1, -1).astype(jnp.bfloat16),
            "seq",
            split_axis=0,
            concat_axis=1,
            tiled=True,
        ),
    )
    d_q_lin, d_gain_query = pull_query(d_q_tok.reshape(tok_rows, H, HD).astype(jnp.float32))
    d_k_lin, d_gain_key = pull_key(d_k_tok.reshape(tok_rows, KV, HD).astype(jnp.float32))
    d_q_low = d_q_lin.astype(jnp.bfloat16)
    d_k_low = d_k_lin.astype(jnp.bfloat16)
    d_v_low = d_v_tok.reshape(tok_rows, -1)
    d_query_w = mat_dot("td,tq->dq", normed_low, d_q_low)
    d_key_w = mat_dot("td,tq->dq", normed_low, d_k_low)
    d_value_w = mat_dot("td,tq->dq", normed_low, d_v_low)
    d_normed = (
        mat_dot("tq,dq->td", d_q_low, query_back)
        + mat_dot("tq,dq->td", d_k_low, key_back)
        + mat_dot("tq,dq->td", d_v_low, value_back)
    )
    d_tok_norm, d_gain_attn = pull_attn_norm(d_normed)
    d_tokens = d_resid + d_tok_norm
    attn_shards = (
        lax.psum_scatter(d_gain_attn, "dp", scatter_dimension=0, tiled=True),
        lax.psum_scatter(d_query_w, "dp", scatter_dimension=0, tiled=True),
        lax.psum_scatter(d_key_w, "dp", scatter_dimension=0, tiled=True),
        lax.psum_scatter(d_value_w, "dp", scatter_dimension=0, tiled=True),
        lax.psum_scatter(d_gain_query, "dp", scatter_dimension=0, tiled=True),
        lax.psum_scatter(d_gain_key, "dp", scatter_dimension=0, tiled=True),
        lax.psum_scatter(d_out_w, "dp", scatter_dimension=0, tiled=True),
    )
    summed = lax.psum(
        (
            attn_shards[0],
            attn_shards[1],
            attn_shards[2],
            attn_shards[3],
            attn_shards[4],
            attn_shards[5],
            attn_shards[6],
            ffn_shards[0],
            ffn_shards[1],
            ffn_shards[2],
            ffn_shards[3],
        ),
        "seq",
    )
    return (
        block_out,
        d_tokens,
        summed[0],
        summed[1],
        summed[2],
        summed[3],
        summed[4],
        summed[5],
        summed[6],
        summed[7],
        summed[8],
        summed[9],
        summed[10],
    )


def solution(mesh):
    return jax.shard_map(
        body,
        mesh=mesh,
        in_specs=(
            P(("dp", "seq"), None),
            P("dp", None),
            P("dp"),
            P("dp", None),
            P("dp", None),
            P("dp", None),
            P("dp"),
            P("dp"),
            P("dp", None),
            P("dp"),
            P("dp", None),
            P("dp", None),
            P("dp", None),
            P(("dp", "seq"), None),
        ),
        out_specs=(
            P(("dp", "seq"), None),
            P(("dp", "seq"), None),
            P("dp"),
            P("dp", None),
            P("dp", None),
            P("dp", None),
            P("dp"),
            P("dp"),
            P("dp", None),
            P("dp"),
            P("dp", None),
            P("dp", None),
            P("dp", None),
        ),
        check_vma=False,
    )
```

profile of v0, /device:TPU:0, one launch (start us, length us, event | category | flops | bytes accessed | tf_op | source)
XLA Modules:
  0.0 1586.6 jit_solution(17672986321578510262)
XLA Ops:
  15.5 36.1 %all-reduce.16 = (bf16[64]{0:T(256)(128)(2,1)S(1)}, bf16[1024]{0:T(1024)(128)(2,1)S(1)}, bf16[64]{0:T(256)(128)(2,1)S(1)}, bf16[1024]{0:T(1024)(128)(2,1)}) all-reduce(bf16[64]{0:T(256)(128)(2,1)S(1)} %dynamic-update-slice.1, bf16[1024]{0:T(1024)(128)(2,1)S(1)} %dynamic-update-slice, ...), channel_id=1, replica_groups=mesh['dp'=16,'seq'=2] {'dp'}, use_global_device_ids=true, to_apply=%add.6 | all-reduce | flops 2176 | bytes 8704
  61.4 28.7 %all-gather.12.cloned.1.call-done = bf16[1024,512]{1,0:T(8,128)(2,1)} async-done(((bf16[64,512]{1,0:T(8,128)(2,1)}), bf16[1024,512]{1,0:T(8,128)(2,1)}) %all-gather.12.cloned.1.call-update) | async-done | bytes 1048592 | tf_op jit(solution)/shard_map/all_gather | solution.py:98
  92.9 39.9 %all-gather.8.cloned.1.call-done = bf16[1024,1024]{1,0:T(8,128)(2,1)} async-done(((bf16[64,1024]{1,0:T(8,128)(2,1)}), bf16[1024,1024]{1,0:T(8,128)(2,1)}) %all-gather.8.cloned.1.call-update) | async-done | bytes 2097168 | tf_op jit(solution)/shard_map/all_gather | solution.py:96
  142.4 7.2 all-to-all-done.2
  149.6 5.0 all-to-all-start
  157.5 10.7 all-to-all-done
  168.3 29.5 %while.28 = (s32[]{:T(128)}, bf16[2,512,4,2,64]{1,4,3,2,0:T(8,128)(2,1)S(1)}, f32[2,4,2,512]{3,2,1,0:T(2,128)S(1)}, s32[2,512]{1,0:T(2,128)S(1)}, s32[2,512]{1,0...) while((s32[]{:T(128)}, ...), condition=%wide.region_7.8_spmd.clone, body=%wide.region_4.7_spmd.clone.sunk | while | flops 1125644288 | bytes 55201920 | solution.py:169
  177.8 5.2 fusion.153
  192.6 5.2 fusion.153
  202.2 7.6 reshape.486
  210.4 8.0 reduce
  224.8 12.5 all-to-all-done.3
  249.8 7.0 all-gather.16.cloned.1.call-done
  256.8 11.0 fusion.78
  267.8 70.4 %all-gather.18.cloned.1.call-done = bf16[1024,4608]{1,0:T(8,128)(2,1)} async-done(((bf16[64,4608]{1,0:T(8,128)(2,1)}), bf16[1024,4608]{1,0:T(8,128)(2,1)}) %all-gather.18.cloned.1.call-update) | async-done | bytes 9437200 | tf_op jit(solution)/shard_map/all_gather | solution.py:106
  338.3 11.1 fusion.79
  349.4 70.5 %all-gather.20.cloned.1.call-done = bf16[4608,1024]{1,0:T(8,128)(2,1)} async-done(((bf16[288,1024]{1,0:T(8,128)(2,1)}), bf16[4608,1024]{1,0:T(8,128)(2,1)}) %all-gather.20.cloned.1.call-update) | async-done | bytes 9437200 | tf_op jit(solution)/shard_map/all_gather | solution.py:107
  419.9 18.5 %multiply_convert_fusion = (bf16[512,4608]{1,0:T(8,128)(2,1)}, bf16[512,4608]{1,0:T(8,128)(2,1)}, bf16[512,4608]{1,0:T(8,128)(2,1)}) fusion(f32[512,4608]{1,0:T(8,128)} %fusion.78, f32[512,4608]{1,0:T(8,128)} %fusion.79, bf16[4608,1024]{1,0:T(8,128)(2,1)} %all-gather.20.cloned.1.call-done, f32[512,1024]{1,0:T(8,128)} %param.31, ...), kind=kOutput, calls=%fused_computation.73 | convolution fusion | flops 4870635520 | bytes 44566528 | tf_op jit(solution)/shard_map/td,fd->tf/dot_general | solution.py:61
  438.4 9.2 fusion.80
  447.6 9.2 multiply_reduce_fusion
  464.4 14.2 all-to-all-done.4
  481.0 87.6 %while.29 = (s32[]{:T(128)}, f32[1024,4,64]{0,2,1:T(8,128)}, f32[1024,4,64]{0,2,1:T(8,128)}, bf16[2,512,4,2,64]{1,4,3,2,0:T(8,128)(2,1)}, bf16[2,512,4,2,64]{1,4...) while((s32[]{:T(128)}, f32[1024,4,64]{0,2,1:T(8,128)}, ...), condition=%wide.region_12.13_spmd.clone, body=%wide.region_10.12_spmd.clone.sunk | while | flops 2725246976 | bytes 186356192 | solution.py:235
  486.5 11.2 fusion.165
  497.7 9.4 fusion.166
  507.1 6.2 fusion.167
  513.4 7.6 fusion.168
  530.3 11.2 fusion.165
  541.4 9.4 fusion.166
  550.8 6.5 fusion.167
  557.3 7.6 fusion.168
  571.4 10.4 all_to_all.108
  590.3 9.4 all_to_all.109
  614.4 7.5 reshape.487
  621.8 8.0 reduce.2
  631.7 15.2 all_to_all.110
  661.4 11.6 fusion.86
  673.1 11.5 fusion.87
  686.2 11.6 fusion.75
  698.1 14.7 reduce-scatter.12.cloned.1.call-done
  712.8 75.4 %reduce-scatter.14.cloned.1.call-done = f32[64,1024]{1,0:T(8,128)} async-done(((f32[1024,1024]{1,0:T(8,128)}), f32[64,1024]{1,0:T(8,128)}) %reduce-scatter.14.cloned.1.call-update) | async-done | bytes 262160 | tf_op jit(solution)/shard_map/reduce_scatter | solution.py:285
  788.2 75.7 %reduce-scatter.8.cloned.1.call-done = f32[64,1024]{1,0:T(8,128)} async-done(((f32[1024,1024]{1,0:T(8,128)}), f32[64,1024]{1,0:T(8,128)}) %reduce-scatter.8.cloned.1.call-update) | async-done | bytes 262160 | tf_op jit(solution)/shard_map/reduce_scatter | solution.py:280
  864.0 197.1 %reduce-scatter.16.cloned.1.call-done = f32[64,4608]{1,0:T(8,128)} async-done(((f32[1024,4608]{1,0:T(8,128)}), f32[64,4608]{1,0:T(8,128)}) %reduce-scatter.16.cloned.1.call-update) | async-done | bytes 1179664 | tf_op jit(solution)/shard_map/reduce_scatter | solution.py:208
  1061.1 197.3 %reduce-scatter.18.cloned.1.call-done = f32[64,4608]{1,0:T(8,128)} async-done(((f32[1024,4608]{1,0:T(8,128)}), f32[64,4608]{1,0:T(8,128)}) %reduce-scatter.18.cloned.1.call-update) | async-done | bytes 1179664 | tf_op jit(solution)/shard_map/reduce_scatter | solution.py:209
  1258.4 197.1 %reduce-scatter.20.cloned.1.call-done = f32[288,1024]{1,0:T(8,128)} async-done(((f32[4608,1024]{1,0:T(8,128)}), f32[288,1024]{1,0:T(8,128)}) %reduce-scatter.20.cloned.1.call-update) | async-done | bytes 1179664 | tf_op jit(solution)/shard_map/reduce_scatter | solution.py:210
  1457.1 10.1 add_multiply_fusion
  1473.6 32.5 %all-reduce.13 = (f32[1024]{0:T(1024)S(1)}, f32[64]{0:T(128)S(1)}, f32[64]{0:T(128)S(1)}, f32[1024]{0:T(1024)S(1)}) all-reduce(f32[1024]{0:T(1024)S(1)} %get-tuple-element.220, f32[64]{0:T(128)S(1)} %get-tuple-element.222, f32[64]{0:T(128)S(1)} %get-tuple-element.224, ...), channel_id=2, replica_groups=mesh['dp'=16,'seq'=2] {'dp'}, use_global_device_ids=true, to_apply=%region_17.18.clone | all-reduce | flops 2176 | bytes 17408
  1506.4 5.5 all-reduce.14
  1516.0 52.5 %all-reduce.19.cloned.1.call-done = (f32[64,1024]{1,0:T(8,128)}, f32[64,512]{1,0:T(8,128)}, f32[64,512]{1,0:T(8,128)}, f32[64,1024]{1,0:T(8,128)}, f32[64,4608]{...) async-done(((f32[64,1024]{1,0:T(8,128)}, f32[64,512]{1,0:T(8,128)}, f32[64,512]{1,0:T(8,128)}, f32[64,1024]{1,0:T(8,128)}, f32[64,4608]{1,0:T(8,128)}, ...) | async-done | bytes 4325392 | tf_op jit(solution)/shard_map/psum | solution.py:287
  (341 shorter events, 168.0 us)
Async XLA Ops:
  7.2 7.4 copy-start.68
  7.2 7.6 copy-start.69
  7.2 7.9 copy-start.70
  7.2 8.1 copy-start.71
  7.2 44.5 %copy-start.4 = (f32[512,1024]{1,0:T(8,128)S(1)}, f32[512,1024]{1,0:T(8,128)}, u32[]{:S(2)}) copy-start(f32[512,1024]{1,0:T(8,128)} %param.18) | copy-start | bytes 6291460
  7.2 46.0 %all-gather.10.cloned.1.call-start = ((), (), s32[]{:S(2)}) async-start(), calls=%async_computation.16 | async-start | bytes 1114112 | tf_op jit(solution)/shard_map/all_gather | solution.py:97
  8.0 82.2 %all-gather.12.cloned.1.call-start = ((), (), s32[]{:S(2)}) async-start(), calls=%async_computation.17 | async-start | bytes 1114112 | tf_op jit(solution)/shard_map/all_gather | solution.py:98
  8.7 124.0 %all-gather.8.cloned.1.call-start = ((), (), s32[]{:S(2)}) async-start(), calls=%async_computation.15 | async-start | bytes 2228224 | tf_op jit(solution)/shard_map/all_gather | solution.py:96
  9.5 235.5 %all-gather.14.cloned.1.call-start = ((), (), s32[]{:S(2)}) async-start(), calls=%async_computation.18 | async-start | bytes 2228224 | tf_op jit(solution)/shard_map/all_gather | solution.py:101
  10.0 246.7 %all-gather.16.cloned.1.call-start = ((), (), s32[]{:S(2)}) async-start(), calls=%async_computation.19 | async-start | bytes 10027008 | tf_op jit(solution)/shard_map/all_gather | solution.py:105
  10.6 327.6 %all-gather.18.cloned.1.call-start = ((), (), s32[]{:S(2)}) async-start(), calls=%async_computation.20 | async-start | bytes 10027008 | tf_op jit(solution)/shard_map/all_gather | solution.py:106
  11.2 408.7 %all-gather.20.cloned.1.call-start = ((), (), s32[]{:S(2)}) async-start(), calls=%async_computation.21 | async-start | bytes 10027008 | tf_op jit(solution)/shard_map/all_gather | solution.py:107
  51.7 84.6 %copy-start.61 = (f32[64]{0:T(128)}, f32[64]{0:T(128)S(1)}, u32[]{:S(2)}) copy-start(f32[64]{0:T(128)S(1)} %convert_element_type.173) | copy-start | bytes 772
  52.8 80.0 %copy-start.15 = (bf16[512,1024]{1,0:T(8,128)(2,1)}, bf16[512,1024]{1,0:T(8,128)(2,1)S(1)}, u32[]{:S(2)}) copy-start(bf16[512,1024]{1,0:T(8,128)(2,1)S(1)} %multiply_convert_fusion.3) | copy-start | bytes 3145732
  53.2 87.8 %copy-start.31 = (f32[512,32]{0,1:T(8,128)}, f32[512,32]{0,1:T(8,128)S(1)}, u32[]{:S(2)}) copy-start(f32[512,32]{0,1:T(8,128)S(1)} %get-tuple-element.306) | copy-start | bytes 196612
  53.2 87.8 %copy-start.33 = (f32[512,32]{0,1:T(8,128)}, f32[512,32]{0,1:T(8,128)S(1)}, u32[]{:S(2)}) copy-start(f32[512,32]{0,1:T(8,128)S(1)} %get-tuple-element.307) | copy-start | bytes 196612
  57.2 80.3 %all-to-all-start.1 = ((bf16[512,2,256]{0,2,1:T(8,128)(2,1)}), bf16[512,2,256]{0,2,1:T(8,128)(2,1)}, u32[]{:S(2)}, u32[]{:S(2)}) async-start(bf16[512,2,256]{0,2,1:T(8,128)(2,1)} %bitcast.10), calls=%async_computation.1 | async-start | bytes 1048576 | tf_op jit(solution)/shard_map/all_to_all | solution.py:133
  137.5 12.1 all-to-all-start.2
  149.6 18.5 %all-to-all-start = ((bf16[512,2,512]{0,2,1:T(8,128)(2,1)}), bf16[512,2,512]{0,2,1:T(8,128)(2,1)}, u32[]{:S(2)}, u32[]{:S(2)}) async-start(bf16[512,2,512]{0,2,1:T(8,128)(2,1)} %bitcast.5), calls=%async_computation | async-start | bytes 2097152 | tf_op jit(solution)/shard_map/all_to_all | solution.py:126
  221.1 16.2 %all-to-all-start.3 = ((bf16[2,2,131072]{2,1,0:T(2,128)(2,1)}), bf16[2,2,131072]{2,1,0:T(2,128)(2,1)S(1)}, u32[]{:S(2)}, u32[]{:S(2)}) async-start(bf16[2,2,131072]{2,1,0:T(2,128)(2,1)} %reshape.492), calls=%async_computation.3 | async-start | bytes 2097152 | tf_op jit(solution)/shard_map/all_to_all | solution.py:171
  224.8 232.0 %copy-start.57 = (f32[512]{0:T(512)}, f32[512]{0:T(512)S(1)}, u32[]{:S(2)}) copy-start(f32[512]{0:T(512)S(1)} %dynamic-slice_convert_fusion.1) | copy-start | bytes 6148
  249.8 88.5 %copy-start.17 = (bf16[512,1024]{1,0:T(8,128)(2,1)}, bf16[512,1024]{1,0:T(8,128)(2,1)S(1)}, u32[]{:S(2)}) copy-start(bf16[512,1024]{1,0:T(8,128)(2,1)S(1)} %multiply_convert_fusion.2) | copy-start | bytes 3145732
  438.4 9.2 copy-start.20
  438.4 9.2 copy-start.24
  447.6 9.2 copy-start.29
  460.8 17.9 %all-to-all-start.4 = ((bf16[512,2,512]{2,0,1:T(8,128)(2,1)}), bf16[512,2,512]{2,0,1:T(8,128)(2,1)S(1)}, u32[]{:S(2)}, u32[]{:S(2)}) async-start(bf16[512,2,512]{2,0,1:T(8,128)(2,1)} %bitcast.213), calls=%async_computation.4 | async-start | bytes 2097152 | tf_op jit(solution)/shard_map/all_to_all | solution.py:216
  464.4 233.8 %reduce-scatter.10.cloned.1.call-start = ((), (), s32[]{:S(2)}) async-start(), calls=%async_computation.23 | async-start | bytes 2228224 | tf_op jit(solution)/shard_map/reduce_scatter | solution.py:281
  507.1 6.3 copy-start
  507.1 6.3 copy-start.1
  507.1 13.9 slice-start
  513.4 7.7 slice-start.1
  513.4 7.7 copy-start.26
  550.8 6.5 copy-start
  550.8 6.5 copy-start.1
  550.8 14.2 slice-start
  557.3 7.7 slice-start.1
  557.3 7.7 copy-start.26
  588.8 124.1 %reduce-scatter.12.cloned.1.call-start = ((), (), s32[]{:S(2)}) async-start(), calls=%async_computation.24 | async-start | bytes 2228224 | tf_op jit(solution)/shard_map/reduce_scatter | solution.py:282
  604.6 183.7 %reduce-scatter.14.cloned.1.call-start = ((), (), s32[]{:S(2)}) async-start(), calls=%async_computation.25 | async-start | bytes 4456448 | tf_op jit(solution)/shard_map/reduce_scatter | solution.py:285
  609.2 254.8 %reduce-scatter.8.cloned.1.call-start = ((), (), s32[]{:S(2)}) async-start(), calls=%async_computation.22 | async-start | bytes 4456448 | tf_op jit(solution)/shard_map/reduce_scatter | solution.py:280
  660.2 400.9 %reduce-scatter.16.cloned.1.call-start = ((), (), s32[]{:S(2)}) async-start(), calls=%async_computation.26 | async-start | bytes 20054016 | tf_op jit(solution)/shard_map/reduce_scatter | solution.py:208
  673.0 585.4 %reduce-scatter.18.cloned.1.call-start = ((), (), s32[]{:S(2)}) async-start(), calls=%async_computation.27 | async-start | bytes 20054016 | tf_op jit(solution)/shard_map/reduce_scatter | solution.py:209
  684.6 770.9 %reduce-scatter.20.cloned.1.call-start = ((), (), s32[]{:S(2)}) async-start(), calls=%async_computation.28 | async-start | bytes 20054016 | tf_op jit(solution)/shard_map/reduce_scatter | solution.py:210
  697.8 870.7 %all-reduce.19.cloned.1.call-start = ((), (), s32[]{:S(2)}) async-start(), calls=%async_computation.29 | async-start | bytes 8650752 | tf_op jit(solution)/shard_map/psum | solution.py:287
  1457.1 10.1 copy-start.23
  1457.1 10.1 copy-start.37
  1471.1 40.8 %copy-start.56 = (f32[512]{0:T(512)S(1)}, f32[512]{0:T(512)}, u32[]{:S(2)}) copy-start(f32[512]{0:T(512)} %copy-done.55) | copy-start | bytes 6148
  1568.5 9.0 copy-start.36
  (56 other events, 116.7 us)
Sparse Core Ops, SparseCore 0:
  10.2 40.6 all-gather.9
  53.1 36.9 all-gather.11
  92.3 40.4 all-gather.7
  134.8 40.1 all-gather.13
  177.1 79.6 all-gather.15
  258.9 79.3 all-gather.17
  340.5 79.3 all-gather.19
  588.9 59.4 reduce-scatter.9
  652.1 60.7 reduce-scatter.11
  716.5 71.6 reduce-scatter.13
  792.1 71.8 reduce-scatter.7
  867.9 193.1 reduce-scatter.15
  1065.2 193.1 reduce-scatter.17
  1262.3 193.0 reduce-scatter.19
  1458.4 110.0 all-reduce.18
where the time goes:
time: 1590 us
  waiting for transfers between devices  1080 us (68%)
  matrix products  215 us (14%)
  blocking collectives  109 us (7%)
  local copies, waits for them, and re-layouts  80.8 us (5%)
  other arithmetic  66.4 us (4%)
  starting transfers between devices  20.7 us (1%)
  between operations  18.9 us (1%)
    reduce_scatter x1, waiting for transfers between devices, body(): lax.psum_scatter(d_up_w, 'dp', scatter_dimension=0, tiled=True)  197 us
    reduce_scatter x1, waiting for transfers between devices, body(): lax.psum_scatter(d_gate_w, 'dp', scatter_dimension=0, tiled=True)  197 us
    reduce_scatter x1, waiting for transfers between devices, body(): lax.psum_scatter(d_down, 'dp', scatter_dimension=0, tiled=True)  197 us
    dot_general x28, matrix products, mat_dot(): return jnp.einsum(form, left, right, preferred_element_type=jnp.float32)  172 us
    reduce_scatter x1, waiting for transfers between devices, body(): lax.psum_scatter(d_query_w, 'dp', scatter_dimension=0, tiled=True)  75.7 us
    reduce_scatter x1, waiting for transfers between devices, body(): lax.psum_scatter(d_out_w, 'dp', scatter_dimension=0, tiled=True)  75.4 us
    all_gather x1, waiting for transfers between devices, body(): lax.all_gather(w_down, 'dp', axis=0, tiled=True)  70.5 us
    all_gather x1, waiting for transfers between devices, body(): lax.all_gather(w_up, 'dp', axis=0, tiled=True)  70.4 us
  transfers between devices with their start and end apart: 20, of which 16 were waited for; matrix products, arithmetic and copies ran while one was open for 13% of the time, Pallas kernels for 0%

commit v1 on v0

--- a/solution.py
+++ b/solution.py
@@ -1,3 +1,4 @@
+import functools
 from functools import partial
 import math
 import jax
@@ -11,6 +12,25 @@
 EPSILON = 1e-05
 ROPE_BASE = 1000000.0
 MASKED_SCORE = -1e30
+
+
+def fill_figure(original, mesh_ax):
+    dev_count = lax.axis_size(mesh_ax)
+    nodes = [(idx, (idx + 1) % dev_count) for idx in range(dev_count)]
+    bank = [(idx, (idx - 1) % dev_count) for idx in range(dev_count)]
+    front, local_now = ([original], [original])
+    for _ in range(dev_count // 2):
+        front.append(lax.ppermute(front[-1], mesh_ax, nodes))
+    for _ in range((dev_count - 1) // 2):
+        local_now.append(lax.ppermute(local_now[-1], mesh_ax, perm=bank))
+    block_now = jnp.concatenate([*front[::-1], *local_now[1:]], axis=0)
+    later = jnp.roll(
+        block_now, (lax.axis_index(mesh_ax) - dev_count // 2) * original.shape[0], axis=0
+    )
+    return later
+
+
+view_kinds = functools.partial(fill_figure, mesh_ax="dp")
 
 
 def rms_norm(values, gain_vec):
@@ -103,7 +123,7 @@
     gain_ffn, gate_full, up_full, down_full = (
         lax.all_gather(ffn_gain, "dp", axis=0, tiled=True),
         lax.all_gather(w_gate, "dp", axis=0, tiled=True),
-        lax.all_gather(w_up, "dp", axis=0, tiled=True),
+        view_kinds(w_up),
         lax.all_gather(w_down, "dp", axis=0, tiled=True),
     )
     normed, pull_attn_norm = jax.vjp(rms_norm, tokens, gain_attn.astype(jnp.float32))

time: 1590 us -> 1630 us (1.025)
  waiting for transfers between devices: 1080 us -> 977 us
  local copies, waits for them, and re-layouts: 80.8 us -> 148 us
  starting transfers between devices: 20.7 us -> 72.3 us
    ppermute x0 -> x15, starting transfers between devices: none -> 52.1 us  [the longest x8 34.3 us: fill_figure(): front.append(lax.ppermute(front[-1], mesh_ax, nodes))]
    unnamed x160 -> x203, local copies, waits for them, and re-layouts: 40.8 us -> 90.9 us
    all_gather x1, waiting for transfers between devices: 28.7 us -> 0.02 us  [body(): lax.all_gather(w_value, 'dp', axis=0, tiled=True)]
    all_gather x1, waiting for transfers between devices: 70.4 us -> 43 us  [body(): lax.all_gather(w_up, 'dp', axis=0, tiled=True)]
    ppermute x0 -> x15, waiting for transfers between devices: none -> 27.2 us  [the longest x8 18 us: fill_figure(): front.append(lax.ppermute(front[-1], mesh_ax, nodes))]
    all_gather x1, waiting for transfers between devices: 39.9 us -> 17 us  [body(): lax.all_gather(w_query, 'dp', axis=0, tiled=True)]
    all_gather x1, waiting for transfers between devices: 70.5 us -> 51.8 us  [body(): lax.all_gather(w_down, 'dp', axis=0, tiled=True)]
  transfers between devices with their start and end apart: 20 -> 35, of which waited for: 16 -> 19; matrix products, arithmetic and copies ran while one was open for 13% -> 18% of each run, Pallas kernels for 0% -> 0%
where the time goes in v1:
time: 1630 us; the launch traced here: 1620 us
  waiting for transfers between devices  977 us (60%)
  matrix products  226 us (14%)
  local copies, waits for them, and re-layouts  148 us (9%)
  blocking collectives  107 us (7%)
  other arithmetic  72.9 us (4%)
  starting transfers between devices  72.3 us (4%)
  between operations  18.9 us (1%)
    reduce_scatter x1, waiting for transfers between devices, body(): lax.psum_scatter(d_up_w, 'dp', scatter_dimension=0, tiled=True)  197 us
    reduce_scatter x1, waiting for transfers between devices, body(): lax.psum_scatter(d_down, 'dp', scatter_dimension=0, tiled=True)  197 us
    reduce_scatter x1, waiting for transfers between devices, body(): lax.psum_scatter(d_gate_w, 'dp', scatter_dimension=0, tiled=True)  197 us
    dot_general x28, matrix products, mat_dot(): return jnp.einsum(form, left, right, preferred_element_type=jnp.float32)  176 us
    unnamed x203, local copies, waits for them, and re-layouts  90.9 us
    reduce_scatter x1, waiting for transfers between devices, body(): lax.psum_scatter(d_query_w, 'dp', scatter_dimension=0, tiled=True)  75.7 us
    reduce_scatter x1, waiting for transfers between devices, body(): lax.psum_scatter(d_out_w, 'dp', scatter_dimension=0, tiled=True)  75.5 us
    unnamed x2, blocking collectives  65.1 us
  transfers between devices with their start and end apart: 35, of which 19 were waited for; matrix products, arithmetic and copies ran while one was open for 18% of the time, Pallas kernels for 0%

profile of v1, /device:TPU:0, one launch (start us, length us, event | category | flops | bytes accessed | tf_op | source)
XLA Modules:
  0.0 1622.2 jit_solution(11033153958591615327)
XLA Ops:
  16.7 7.8 collective-permute-done
  29.9 7.7 collective-permute-done.1
  37.6 9.2 collective-permute-start.2
  52.8 32.6 %all-reduce.16 = (bf16[64]{0:T(256)(128)(2,1)S(1)}, bf16[1024]{0:T(1024)(128)(2,1)S(1)}, bf16[64]{0:T(256)(128)(2,1)S(1)}, bf16[1024]{0:T(1024)(128)(2,1)S(1)}) all-reduce(bf16[64]{0:T(256)(128)(2,1)S(1)} %dynamic-update-slice.1, bf16[1024]{0:T(1024)(128)(2,1)S(1)} %dynamic-update-slice, ...), channel_id=1, replica_groups=mesh['dp'=16,'seq'=2] {'dp'}, use_global_device_ids=true, to_apply=%add.6 | all-reduce | flops 2176 | bytes 8704
  88.6 8.8 collective-permute-done.10
  115.9 7.3 collective-permute-start.5
  134.3 8.5 collective-permute-start.6
  142.8 17.0 %all-gather.8.cloned.1.call-done = bf16[1024,1024]{1,0:T(8,128)(2,1)} async-done(((bf16[64,1024]{1,0:T(8,128)(2,1)}), bf16[1024,1024]{1,0:T(8,128)(2,1)}) %all-gather.8.cloned.1.call-update) | async-done | bytes 2097168 | tf_op jit(solution)/shard_map/all_gather | solution.py:116
  169.5 7.2 all-to-all-done.2
  186.3 7.5 all-to-all-done
  193.9 27.2 %while.28 = (s32[]{:T(128)}, bf16[2,512,4,2,64]{1,4,3,2,0:T(8,128)(2,1)S(1)}, f32[2,4,2,512]{3,2,1,0:T(2,128)S(1)}, s32[2,512]{1,0:T(2,128)S(1)}, s32[2,512]{1,0...) while((s32[]{:T(128)}, ...), condition=%wide.region_7.8_spmd.clone, body=%wide.region_4.7_spmd.clone.sunk | while | flops 1125644288 | bytes 55201912 | solution.py:189
  225.0 9.0 reshape.486
  234.5 8.1 reduce
  310.4 11.4 fusion.81
  321.8 51.8 %all-gather.18.cloned.1.call-done = bf16[4608,1024]{1,0:T(8,128)(2,1)} async-done(((bf16[288,1024]{1,0:T(8,128)(2,1)}), bf16[4608,1024]{1,0:T(8,128)(2,1)}) %all-gather.18.cloned.1.call-update) | async-done | bytes 9437200 | tf_op jit(solution)/shard_map/all_gather | solution.py:127
  373.6 11.7 fusion.79
  385.3 16.9 %multiply_convert_fusion = (bf16[512,4608]{1,0:T(8,128)(2,1)}, bf16[512,4608]{1,0:T(8,128)(2,1)}, bf16[512,4608]{1,0:T(8,128)(2,1)}) fusion(f32[512,4608]{1,0:T(8,128)} %fusion.79, f32[512,4608]{1,0:T(8,128)} %fusion.81, bf16[512,1024]{1,0:T(8,128)(2,1)S(1)} %multiply_convert_fusion.2, bf16[2048,4608]{1,0:T(8,128)(2,1)} %constant_dynamic-update-slice_fusion, ...), kind=kOutput, calls=%fused_computation.73 | convolution fusion | flops 4869586944 | bytes 43515908 | tf_op jit(solution)/shard_map/dot_general | solution.py:198
  402.2 10.0 fusion.82
  412.3 43.0 %all-gather.20.cloned.1.call-done = bf16[1024,4608]{1,0:T(8,128)(2,1)} async-done(((bf16[64,4608]{1,0:T(8,128)(2,1)}), bf16[1024,4608]{1,0:T(8,128)(2,1)}) %all-gather.20.cloned.1.call-update) | async-done | bytes 9437200 | tf_op jit(solution)/shard_map/all_gather | solution.py:212
  455.3 11.2 multiply_reduce_fusion
  475.3 14.3 all-to-all-done.4
  492.2 109.8 %while.29 = (s32[]{:T(128)}, f32[1024,4,64]{0,2,1:T(8,128)}, f32[1024,4,64]{0,2,1:T(8,128)}, bf16[2,512,4,2,64]{1,4,3,2,0:T(8,128)(2,1)}, bf16[2,512,4,2,64]{1,4...) while((s32[]{:T(128)}, f32[1024,4,64]{0,2,1:T(8,128)}, ...), condition=%wide.region_12.13_spmd.clone, body=%wide.region_10.12_spmd.clone.sunk | while | flops 2725246976 | bytes 286889792 | solution.py:255
  493.5 9.2 fusion.163
  504.1 10.1 fusion.166
  519.9 9.9 fusion.167
  536.1 7.7 fusion.170
  547.7 9.2 fusion.163
  558.2 10.1 fusion.166
  574.1 9.9 fusion.167
  584.0 6.5 fusion.168
  590.5 7.7 fusion.170
  604.8 10.7 all_to_all.108
  626.1 10.1 all_to_all.109
  655.8 7.5 reshape.487
  663.2 8.0 reduce.2
  673.1 15.2 all_to_all.110
  703.3 11.8 fusion.88
  715.1 11.6 fusion.89
  728.4 11.5 fusion.78
  740.2 8.4 reduce-scatter.12.cloned.1.call-done
  748.5 75.5 %reduce-scatter.14.cloned.1.call-done = f32[64,1024]{1,0:T(8,128)} async-done(((f32[1024,1024]{1,0:T(8,128)}), f32[64,1024]{1,0:T(8,128)}) %reduce-scatter.14.cloned.1.call-update) | async-done | bytes 262160 | tf_op jit(solution)/shard_map/reduce_scatter | solution.py:305
  824.0 75.7 %reduce-scatter.8.cloned.1.call-done = f32[64,1024]{1,0:T(8,128)} async-done(((f32[1024,1024]{1,0:T(8,128)}), f32[64,1024]{1,0:T(8,128)}) %reduce-scatter.8.cloned.1.call-update) | async-done | bytes 262160 | tf_op jit(solution)/shard_map/reduce_scatter | solution.py:300
  899.7 197.1 %reduce-scatter.16.cloned.1.call-done = f32[64,4608]{1,0:T(8,128)} async-done(((f32[1024,4608]{1,0:T(8,128)}), f32[64,4608]{1,0:T(8,128)}) %reduce-scatter.16.cloned.1.call-update) | async-done | bytes 1179664 | tf_op jit(solution)/shard_map/reduce_scatter | solution.py:228
  1096.8 197.3 %reduce-scatter.18.cloned.1.call-done = f32[64,4608]{1,0:T(8,128)} async-done(((f32[1024,4608]{1,0:T(8,128)}), f32[64,4608]{1,0:T(8,128)}) %reduce-scatter.18.cloned.1.call-update) | async-done | bytes 1179664 | tf_op jit(solution)/shard_map/reduce_scatter | solution.py:229
  1294.0 197.1 %reduce-scatter.20.cloned.1.call-done = f32[288,1024]{1,0:T(8,128)} async-done(((f32[4608,1024]{1,0:T(8,128)}), f32[288,1024]{1,0:T(8,128)}) %reduce-scatter.20.cloned.1.call-update) | async-done | bytes 1179664 | tf_op jit(solution)/shard_map/reduce_scatter | solution.py:230
  1492.5 10.1 add_multiply_fusion
  1507.9 32.5 %all-reduce.13 = (f32[1024]{0:T(1024)S(1)}, f32[64]{0:T(128)S(1)}, f32[64]{0:T(128)S(1)}, f32[1024]{0:T(1024)S(1)}) all-reduce(f32[1024]{0:T(1024)S(1)} %get-tuple-element.220, f32[64]{0:T(128)S(1)} %get-tuple-element.222, f32[64]{0:T(128)S(1)} %get-tuple-element.224, ...), channel_id=2, replica_groups=mesh['dp'=16,'seq'=2] {'dp'}, use_global_device_ids=true, to_apply=%region_17.18.clone | all-reduce | flops 2176 | bytes 17408
  1550.4 53.8 %all-reduce.19.cloned.1.call-done = (f32[64,1024]{1,0:T(8,128)}, f32[64,512]{1,0:T(8,128)}, f32[64,512]{1,0:T(8,128)}, f32[64,1024]{1,0:T(8,128)}, f32[64,4608]{...) async-done(((f32[64,1024]{1,0:T(8,128)}, f32[64,512]{1,0:T(8,128)}, f32[64,512]{1,0:T(8,128)}, f32[64,1024]{1,0:T(8,128)}, f32[64,4608]{1,0:T(8,128)}, ...) | async-done | bytes 4325392 | tf_op jit(solution)/shard_map/psum | solution.py:307
  (397 shorter events, 288.0 us)
Async XLA Ops:
  7.2 81.1 %copy-start.7 = (f32[512,1024]{1,0:T(8,128)S(1)}, f32[512,1024]{1,0:T(8,128)}, u32[]{:S(2)}) copy-start(f32[512,1024]{1,0:T(8,128)} %param.18) | copy-start | bytes 6291460
  7.2 98.9 %all-gather.10.cloned.1.call-start = ((), (), s32[]{:S(2)}) async-start(), calls=%async_computation.16 | async-start | bytes 1114112 | tf_op jit(solution)/shard_map/all_gather | solution.py:117
  7.9 120.6 %all-gather.12.cloned.1.call-start = ((), (), s32[]{:S(2)}) async-start(), calls=%async_computation.17 | async-start | bytes 1114112 | tf_op jit(solution)/shard_map/all_gather | solution.py:118
  8.7 151.2 %all-gather.8.cloned.1.call-start = ((), (), s32[]{:S(2)}) async-start(), calls=%async_computation.15 | async-start | bytes 2228224 | tf_op jit(solution)/shard_map/all_gather | solution.py:116
  9.4 295.4 %all-gather.14.cloned.1.call-start = ((), (), s32[]{:S(2)}) async-start(), calls=%async_computation.18 | async-start | bytes 2228224 | tf_op jit(solution)/shard_map/all_gather | solution.py:121
  10.0 300.4 %all-gather.16.cloned.1.call-start = ((), (), s32[]{:S(2)}) async-start(), calls=%async_computation.19 | async-start | bytes 10027008 | tf_op jit(solution)/shard_map/all_gather | solution.py:125
  10.6 363.0 %all-gather.18.cloned.1.call-start = ((), (), s32[]{:S(2)}) async-start(), calls=%async_computation.20 | async-start | bytes 10027008 | tf_op jit(solution)/shard_map/all_gather | solution.py:127
  11.1 13.4 collective-permute-start
  11.7 17.6 %collective-permute-start.8 = (bf16[64,4608]{1,0:T(8,128)(2,1)}, bf16[64,4608]{1,0:T(8,128)(2,1)S(1)}, u32[]{:S(2)}, u32[]{:S(2)}) collective-permute-start(bf16[64,4608]{1,0:T(8,128)(2,1)} %param.29), channel_id=1, source_target_pairs={{0,30},{2,0},{4,2},{6,4},{8,6},{10,8},{12,10},{14,12},{16,14},{18,... | collective-permute-start | bytes 1769480 | tf_op jit(solution)/shard_map/ppermute | solution.py:25
  24.5 13.1 collective-permute-start.1
  29.3 58.7 %copy-start.29 = (bf16[64,4608]{1,0:T(8,128)(2,1)}, bf16[64,4608]{1,0:T(8,128)(2,1)S(1)}, u32[]{:S(2)}) copy-start(bf16[64,4608]{1,0:T(8,128)(2,1)S(1)} %collective-permute-done.8) | copy-start | bytes 1769476
  29.3 58.1 %collective-permute-start.9 = (bf16[64,4608]{1,0:T(8,128)(2,1)S(1)}, bf16[64,4608]{1,0:T(8,128)(2,1)}, u32[]{:S(2)}, u32[]{:S(2)}) collective-permute-start(bf16[64,4608]{1,0:T(8,128)(2,1)S(1)} %collective-permute-done.8), channel_id=1, source_target_pairs={{0,30},{2,0},{4,2},{6,4},{8,6},{10,8},{12,10},{14,12},{16,14},{18,... | collective-permute-start | bytes 1769480 | tf_op jit(solution)/shard_map/ppermute | solution.py:25
  37.6 50.4 %copy-start.33 = (bf16[64,4608]{1,0:T(8,128)(2,1)}, bf16[64,4608]{1,0:T(8,128)(2,1)S(1)}, u32[]{:S(2)}) copy-start(bf16[64,4608]{1,0:T(8,128)(2,1)S(1)} %collective-permute-done.1) | copy-start | bytes 1769476
  37.6 49.9 %collective-permute-start.2 = (bf16[64,4608]{1,0:T(8,128)(2,1)S(1)}, bf16[64,4608]{1,0:T(8,128)(2,1)}, u32[]{:S(2)}, u32[]{:S(2)}) collective-permute-start(bf16[64,4608]{1,0:T(8,128)(2,1)S(1)} %collective-permute-done.1), channel_id=1, source_target_pairs={{0,2},{2,4},{4,6},{6,8},{8,10},{10,12},{12,14},{14,16},{16,18},{18... | collective-permute-start | bytes 1769480 | tf_op jit(solution)/shard_map/ppermute | solution.py:23
  85.5 77.4 %copy-start.71 = (f32[64]{0:T(128)}, f32[64]{0:T(128)S(1)}, u32[]{:S(2)}) copy-start(f32[64]{0:T(128)S(1)} %convert_element_type.173) | copy-start | bytes 772
  87.4 10.0 collective-permute-start.10
  87.5 14.6 collective-permute-start.3
  88.3 79.8 %copy-start.41 = (f32[512,32]{0,1:T(8,128)}, f32[512,32]{0,1:T(8,128)S(1)}, u32[]{:S(2)}) copy-start(f32[512,32]{0,1:T(8,128)S(1)} %get-tuple-element.306) | copy-start | bytes 196612
  88.3 79.8 %copy-start.43 = (f32[512,32]{0,1:T(8,128)}, f32[512,32]{0,1:T(8,128)S(1)}, u32[]{:S(2)}) copy-start(f32[512,32]{0,1:T(8,128)S(1)} %get-tuple-element.307) | copy-start | bytes 196612
  88.6 71.3 %copy-start.16 = (bf16[512,1024]{1,0:T(8,128)(2,1)}, bf16[512,1024]{1,0:T(8,128)(2,1)S(1)}, u32[]{:S(2)}) copy-start(bf16[512,1024]{1,0:T(8,128)(2,1)S(1)} %multiply_convert_fusion.3) | copy-start | bytes 3145732
  97.4 12.3 collective-permute-start.11
  102.1 13.9 collective-permute-start.4
  108.2 54.6 %copy-start.53 = (f32[512,8]{0,1:T(8,128)}, f32[512,8]{0,1:T(8,128)S(1)}, u32[]{:S(2)}) copy-start(f32[512,8]{0,1:T(8,128)S(1)} %fusion.72) | copy-start | bytes 49156
  109.8 53.0 %copy-start.35 = (bf16[64,4608]{1,0:T(8,128)(2,1)}, bf16[64,4608]{1,0:T(8,128)(2,1)S(1)}, u32[]{:S(2)}) copy-start(bf16[64,4608]{1,0:T(8,128)(2,1)S(1)} %collective-permute-done.11) | copy-start | bytes 1769476
  109.8 21.6 %collective-permute-start.12 = (bf16[64,4608]{1,0:T(8,128)(2,1)S(1)}, bf16[64,4608]{1,0:T(8,128)(2,1)}, u32[]{:S(2)}, u32[]{:S(2)}) collective-permute-start(bf16[64,4608]{1,0:T(8,128)(2,1)S(1)} %collective-permute-done.11), channel_id=1, source_target_pairs={{0,30},{2,0},{4,2},{6,4},{8,6},{10,8},{12,10},{14,12},{16,14},{18,... | collective-permute-start | bytes 1769480 | tf_op jit(solution)/shard_map/ppermute | solution.py:25
  115.9 46.8 %copy-start.37 = (bf16[64,4608]{1,0:T(8,128)(2,1)}, bf16[64,4608]{1,0:T(8,128)(2,1)S(1)}, u32[]{:S(2)}) copy-start(bf16[64,4608]{1,0:T(8,128)(2,1)S(1)} %collective-permute-done.4) | copy-start | bytes 1769476
  115.9 18.4 %collective-permute-start.5 = (bf16[64,4608]{1,0:T(8,128)(2,1)S(1)}, bf16[64,4608]{1,0:T(8,128)(2,1)}, u32[]{:S(2)}, u32[]{:S(2)}) collective-permute-start(bf16[64,4608]{1,0:T(8,128)(2,1)S(1)} %collective-permute-done.4), channel_id=1, source_target_pairs={{0,2},{2,4},{4,6},{6,8},{8,10},{10,12},{12,14},{14,16},{16,18},{18... | collective-permute-start | bytes 1769480 | tf_op jit(solution)/shard_map/ppermute | solution.py:23
  124.3 40.3 %all-to-all-start.1 = ((bf16[512,2,256]{0,2,1:T(8,128)(2,1)}), bf16[512,2,256]{0,2,1:T(8,128)(2,1)}, u32[]{:S(2)}, u32[]{:S(2)}) async-start(bf16[512,2,256]{0,2,1:T(8,128)(2,1)} %bitcast.10), calls=%async_computation.1 | async-start | bytes 1048576 | tf_op jit(solution)/shard_map/all_to_all | solution.py:153
  131.3 53.9 %collective-permute-start.13 = (bf16[64,4608]{1,0:T(8,128)(2,1)}, bf16[64,4608]{1,0:T(8,128)(2,1)}, u32[]{:S(2)}, u32[]{:S(2)}) collective-permute-start(bf16[64,4608]{1,0:T(8,128)(2,1)} %collective-permute-done.12), channel_id=1, source_target_pairs={{0,30},{2,0},{4,2},{6,4},{8,6},{10,8},{12,10},{14,12},{16,14},{18,... | collective-permute-start | bytes 1769480 | tf_op jit(solution)/shard_map/ppermute | solution.py:25
  134.3 51.8 %collective-permute-start.6 = (bf16[64,4608]{1,0:T(8,128)(2,1)}, bf16[64,4608]{1,0:T(8,128)(2,1)}, u32[]{:S(2)}, u32[]{:S(2)}) collective-permute-start(bf16[64,4608]{1,0:T(8,128)(2,1)} %collective-permute-done.5), channel_id=1, source_target_pairs={{0,2},{2,4},{4,6},{6,8},{8,10},{10,12},{12,14},{14,16},{16,18},{18... | collective-permute-start | bytes 1769480 | tf_op jit(solution)/shard_map/ppermute | solution.py:23
  164.6 12.1 all-to-all-start.2
  176.7 17.1 %all-to-all-start = ((bf16[512,2,512]{0,2,1:T(8,128)(2,1)}), bf16[512,2,512]{0,2,1:T(8,128)(2,1)S(1)}, u32[]{:S(2)}, u32[]{:S(2)}) async-start(bf16[512,2,512]{0,2,1:T(8,128)(2,1)} %bitcast.5), calls=%async_computation | async-start | bytes 2097152 | tf_op jit(solution)/shard_map/all_to_all | solution.py:146
  180.3 274.9 %all-gather.20.cloned.1.call-start = ((), (), s32[]{:S(2)}) async-start(), calls=%async_computation.21 | async-start | bytes 10027008 | tf_op jit(solution)/shard_map/all_gather | solution.py:212
  185.3 86.6 %collective-permute-start.14 = (bf16[64,4608]{1,0:T(8,128)(2,1)}, bf16[64,4608]{1,0:T(8,128)(2,1)}, u32[]{:S(2)}, u32[]{:S(2)}) collective-permute-start(bf16[64,4608]{1,0:T(8,128)(2,1)} %collective-permute-done.13), channel_id=1, source_target_pairs={{0,30},{2,0},{4,2},{6,4},{8,6},{10,8},{12,10},{14,12},{16,14},{18,... | collective-permute-start | bytes 1769480 | tf_op jit(solution)/shard_map/ppermute | solution.py:25
  186.1 61.7 %collective-permute-start.7 = (bf16[64,4608]{1,0:T(8,128)(2,1)}, bf16[64,4608]{1,0:T(8,128)(2,1)}, u32[]{:S(2)}, u32[]{:S(2)}) collective-permute-start(bf16[64,4608]{1,0:T(8,128)(2,1)} %collective-permute-done.6), channel_id=1, source_target_pairs={{0,2},{2,4},{4,6},{6,8},{8,10},{10,12},{12,14},{14,16},{16,18},{18... | collective-permute-start | bytes 1769480 | tf_op jit(solution)/shard_map/ppermute | solution.py:23
  244.1 54.2 %all-to-all-start.3 = ((bf16[2,2,131072]{2,1,0:T(2,128)(2,1)}), bf16[2,2,131072]{2,1,0:T(2,128)(2,1)S(1)}, u32[]{:S(2)}, u32[]{:S(2)}) async-start(bf16[2,2,131072]{2,1,0:T(2,128)(2,1)} %reshape.492), calls=%async_computation.3 | async-start | bytes 2097152 | tf_op jit(solution)/shard_map/all_to_all | solution.py:191
  310.4 74.9 %copy-start.18 = (bf16[512,1024]{1,0:T(8,128)(2,1)}, bf16[512,1024]{1,0:T(8,128)(2,1)S(1)}, u32[]{:S(2)}) copy-start(bf16[512,1024]{1,0:T(8,128)(2,1)S(1)} %multiply_convert_fusion.2) | copy-start | bytes 3145732
  310.4 63.2 %copy-start.67 = (f32[512]{0:T(512)S(1)}, f32[512]{0:T(512)}, u32[]{:S(2)}) copy-start(f32[512]{0:T(512)} %dynamic-slice_convert_fusion.1) | copy-start | bytes 6148
  470.8 18.8 %all-to-all-start.4 = ((bf16[512,2,512]{2,0,1:T(8,128)(2,1)}), bf16[512,2,512]{2,0,1:T(8,128)(2,1)}, u32[]{:S(2)}, u32[]{:S(2)}) async-start(bf16[512,2,512]{2,0,1:T(8,128)(2,1)} %bitcast.212), calls=%async_computation.4 | async-start | bytes 2097152 | tf_op jit(solution)/shard_map/all_to_all | solution.py:236
  475.3 264.9 %reduce-scatter.10.cloned.1.call-start = ((), (), s32[]{:S(2)}) async-start(), calls=%async_computation.23 | async-start | bytes 2228224 | tf_op jit(solution)/shard_map/reduce_scatter | solution.py:301
  624.5 124.0 %reduce-scatter.12.cloned.1.call-start = ((), (), s32[]{:S(2)}) async-start(), calls=%async_computation.24 | async-start | bytes 2228224 | tf_op jit(solution)/shard_map/reduce_scatter | solution.py:302
  646.0 178.0 %reduce-scatter.14.cloned.1.call-start = ((), (), s32[]{:S(2)}) async-start(), calls=%async_computation.25 | async-start | bytes 4456448 | tf_op jit(solution)/shard_map/reduce_scatter | solution.py:305
  650.6 249.1 %reduce-scatter.8.cloned.1.call-start = ((), (), s32[]{:S(2)}) async-start(), calls=%async_computation.22 | async-start | bytes 4456448 | tf_op jit(solution)/shard_map/reduce_scatter | solution.py:300
  703.2 393.6 %reduce-scatter.16.cloned.1.call-start = ((), (), s32[]{:S(2)}) async-start(), calls=%async_computation.26 | async-start | bytes 20054016 | tf_op jit(solution)/shard_map/reduce_scatter | solution.py:228
  715.1 578.9 %reduce-scatter.18.cloned.1.call-start = ((), (), s32[]{:S(2)}) async-start(), calls=%async_computation.27 | async-start | bytes 20054016 | tf_op jit(solution)/shard_map/reduce_scatter | solution.py:229
  726.8 764.4 %reduce-scatter.20.cloned.1.call-start = ((), (), s32[]{:S(2)}) async-start(), calls=%async_computation.28 | async-start | bytes 20054016 | tf_op jit(solution)/shard_map/reduce_scatter | solution.py:230
  739.8 752.7 %copy-start.22 = (f32[512,1024]{1,0:T(8,128)S(1)}, f32[512,1024]{1,0:T(8,128)}, u32[]{:S(2)}) copy-start(f32[512,1024]{1,0:T(8,128)} %copy-done.20) | copy-start | bytes 6291460
  739.8 864.3 %all-reduce.19.cloned.1.call-start = ((), (), s32[]{:S(2)}) async-start(), calls=%async_computation.29 | async-start | bytes 8650752 | tf_op jit(solution)/shard_map/psum | solution.py:307
  (69 other events, 610.0 us)
Sparse Core Ops, SparseCore 0:
  10.2 50.2 all-gather.9
  62.6 41.5 all-gather.11
  106.4 53.3 all-gather.7
  161.9 48.2 all-gather.13
  212.2 79.8 all-gather.15
  294.3 79.3 all-gather.17
  375.9 79.3 all-gather.19
  624.6 59.2 reduce-scatter.9
  687.7 60.7 reduce-scatter.11
  752.2 71.7 reduce-scatter.13
  827.9 71.8 reduce-scatter.7
  903.7 193.0 reduce-scatter.15
  1100.9 193.1 reduce-scatter.17
  1298.0 193.1 reduce-scatter.19
  1494.1 110.0 all-reduce.18
